TPU v7x, 32 devices: a 4x4x1 block of a 4x4x8 slice. The times are simulated.
32 devices in a mesh: batch: 1 (over z), rows: 4 (over y), ksplit: 8 (over x, core).
Axes of the slice: x: 4, y: 4, z: 1, core: 2. Of those that a mesh axis runs over, the one named last changes fastest.
The devices are a block of a 4x4x8 slice.
Arguments:
- a_vals: bfloat16 [4, 8, 12, 128, 128], P(('batch', 'rows'), 'ksplit')
- b_vals: bfloat16 [8, 72, 128, 128], P(('batch', 'ksplit'))
- pairs: int32 [4, 8, 432, 1, 2], P(('batch', 'rows'), 'ksplit')
- plist_idx: int32 [4, 8, 432, 2], P(('batch', 'rows'), 'ksplit')
- c_idx: int32 [4, 8, 72, 2], P(('batch', 'rows'), 'ksplit')
Outputs:
- output: float32 [4, 8, 72, 128, 128], P(('batch', 'rows'), 'ksplit')
All inputs are finite; a program needn't handle non-finite values.
Results may differ from a plain program's by a relative error of at most 0.001.
Values are sent between devices in bfloat16 or wider.
A program may use at most 768 MiB of HBM per device.

v0:
```python
import functools

import jax
import jax.numpy as jnp
from jax import lax
from jax.experimental import pallas as pl
from jax.experimental.pallas import tpu as pltpu
from jax.sharding import PartitionSpec as P

MESH = pl.DeviceIdType.MESH
RING = 4
HALF_CHUNKS = (3, 3, 3, 2, 2)
LEFT, RIGHT, FAR = 3, 1, 2


def plan(nb):
    half = sum(HALF_CHUNKS)
    quad = (nb - 4 * half) // RING
    assert 4 * half + RING * quad == nb
    return half, quad


def kernel(na, nb, nc, head, a_hbm, b_hbm, pairs_hbm, plist_hbm, cidx_hbm, acc, far_twin, far_tab, *scratch):
    mine, twin = scratch[0:RING], list(scratch[RING:2 * RING - 1])
    twin.insert(FAR, far_twin)
    (meta, cidx, tab_v, tab_s, loc_sem, link_sem, recv_sem, dsend, drecv, msem) = scratch[2 * RING - 1:]
    half, quad = plan(nb)
    nk, ah = len(HALF_CHUNKS), na // 2
    parts = ((0, quad // 2), (quad // 2, quad - quad // 2))
    offs = [(sum(HALF_CHUNKS[:k]), HALF_CHUNKS[k]) for k in range(nk)]
    ks = lax.axis_index("ksplit")
    y = lax.axis_index("rows")
    core = ks % 2
    x = ks // 2

    def chip(dx, flip=0):
        return {"ksplit": ((x + dx) % RING) * 2 + (1 - core if flip else core)}

    sib = chip(0, 1)
    links = {
        "x+": (0, chip(1)), "x-": (1, chip(3)),
        "y+": (2, {"rows": (y + 1) % RING}), "y-": (3, {"rows": (y + 3) % RING}),
    }

    loads = [
        pltpu.make_async_copy(b_hbm, mine[0].at[pl.ds(0, nb)], loc_sem.at[0]),
        pltpu.make_async_copy(a_hbm, mine[0].at[pl.ds(nb, na)], loc_sem.at[1]),
        pltpu.make_async_copy(pairs_hbm, meta.at[0, 0], loc_sem.at[2]),
        pltpu.make_async_copy(plist_hbm, meta.at[0, 1], loc_sem.at[2]),
        pltpu.make_async_copy(cidx_hbm, cidx, loc_sem.at[3]),
    ]
    for load in loads:
        load.start()

    barrier = pltpu.get_barrier_semaphore()
    devices = [dev for _, dev in links.values()] + [chip(2), sib]
    for dev in devices:
        pl.semaphore_signal(barrier, inc=1, device_id=dev, device_id_type=MESH)
    zero = jnp.zeros(mine[0].shape[1:], mine[0].dtype)
    for ref in (*mine, *twin):
        ref[nb + na] = zero
    with jax.named_scope('barrier'):
        pl.semaphore_wait(barrier, len(devices))

    sems = {}
    load_of = {}
    link_of = [0] * len(links)

    def index(key):
        return sems.setdefault(key, len(sems))

    def send(link, key, src, dst, start, size):
        slot, dev = links[link]
        n = index(key)
        load_of[n] = load_of.get(n, 0) + size
        link_of[slot] += size
        pltpu.make_async_remote_copy(
            src_ref=mine[src].at[pl.ds(start, size)], dst_ref=mine[dst].at[pl.ds(start, size)],
            send_sem=link_sem.at[slot], recv_sem=recv_sem.at[n],
            device_id=dev, device_id_type=MESH).start()

    def take(size, sem):
        view = mine[0].at[pl.ds(0, size)]
        pltpu.make_async_copy(view, view, sem).wait()

    waited = {}

    def arrive(key, size):
        n = index(key)
        waited[n] = waited.get(n, 0) + size
        with jax.named_scope('_'.join(str(t) for t in key).replace('+', 'p').replace('-', 'm').replace(' ', '')):
            take(size, recv_sem.at[n])

    def share(d, start, size):
        pltpu.make_async_remote_copy(
            src_ref=mine[d].at[pl.ds(start, size)], dst_ref=twin[d].at[pl.ds(start, size)],
            send_sem=dsend.at[d], recv_sem=drecv.at[d], device_id=sib, device_id_type=MESH).start()

    own = (y % 2) * (2 * half)
    theirs = (1 - y % 2) * (2 * half)

    def quad_at(dy):
        return 4 * half + ((y + dy) % RING) * quad

    def lay(k, base):
        off, size = offs[k]
        return base + off, base + half + off, size

    q0, qm, qp, qf = quad_at(0), quad_at(3), quad_at(1), quad_at(2)

    loads[0].wait()
    def pieces(first, second):
        (off, size), rest = parts[first], parts[second]
        return ((off, 1, "f"), (off + 1, size - 1, "f"), (*rest, ""))

    w_pieces = list(zip(pieces(0, 1), pieces(1, 0)))
    for n, pair in enumerate(w_pieces):
        for link, d, (off, size, _) in zip(("x+", "x-"), (LEFT, RIGHT), pair):
            send(link, ("xw", n), 0, d, q0 + off, size)
    pltpu.make_async_copy(meta.at[0], meta.at[0], loc_sem.at[2]).wait()

    def list_to(slot, src, dev, sem):
        pltpu.make_async_remote_copy(
            src_ref=meta.at[src], dst_ref=meta.at[slot], send_sem=msem.at[0], recv_sem=msem.at[sem],
            device_id=dev, device_id_type=MESH).start()

    def lists_taken(count, sem):
        view = meta.at[pl.ds(0, count)]
        pltpu.make_async_copy(view, view, msem.at[sem]).wait()

    for dx in range(1, RING):
        list_to(2 * (RING - dx), 0, chip(dx), 1)
    list_to(1, 0, sib, 2)
    for k in range(nk):
        u, v, size = lay(k, own)
        send("x+", ("x", k, 0), 0, LEFT, u, size)
        send("x-", ("x", k, 0), 0, RIGHT, v, size)
        send("x+", ("x", k, 1), 0, LEFT, v, size)
        send("x-", ("x", k, 1), 0, RIGHT, u, size)
    loads[1].wait()

    def build_table():
      with jax.named_scope('table'):
            loads[4].wait()
            lists_taken(RING, 2)
            npart = meta.shape[3]
            ckey = cidx[0:1, :] * 4096 + cidx[1:2, :]
            eye = lax.broadcasted_iota(jnp.int32, (nc, nc), 0) == lax.broadcasted_iota(jnp.int32, (nc, nc), 1)
            ccol = jnp.sum(jnp.where(eye, jnp.broadcast_to(ckey, (nc, nc)), 0), axis=1, keepdims=True)
            lane = lax.broadcasted_iota(jnp.int32, (nc, 128), 1)
            table = jnp.zeros((nc, 128), jnp.int32)
            for slot in range(2 * RING):
                pkey = meta[slot, 1, 0:1, :] * 4096 + meta[slot, 1, 1:2, :]
                pval = meta[slot, 0, 0:1, :] * 4096 + meta[slot, 0, 1:2, :] - na * 4096
                hit = jnp.broadcast_to(ccol, (nc, npart)) == jnp.broadcast_to(pkey, (nc, npart))
                found = jnp.sum(jnp.where(hit, jnp.broadcast_to(pval, (nc, npart)), 0), axis=1, keepdims=True) + na * 4096
                a_at = nb + jnp.clip(lax.shift_right_arithmetic(found, 12), 0, na)
                b_at = jnp.clip(found & 4095, 0, nb - 1)
                table = jnp.where(lane == 2 * slot, a_at, table)
                table = jnp.where(lane == 2 * slot + 1, b_at, table)
                if slot == 2 * FAR + 1:
                    for n, column in enumerate((a_at, b_at)):
                        row = jnp.sum(jnp.where(eye, jnp.broadcast_to(column, (nc, nc)), 0), axis=0, keepdims=True)
                        far_tab[n:n + 1, 0:nc] = row
            tab_v[...] = table
            pltpu.make_async_copy(tab_v, tab_s, loc_sem.at[3]).start()

    def stage(d, sides=(0, 1), lo=0, hi=nc, group=24, first=False):
        def product(side, c):
            ref, n = (twin if side else mine)[d], 4 * d + 2 * side
            p = jnp.dot(ref[tab_s[c, n]], ref[tab_s[c, n + 1]], preferred_element_type=jnp.float32)
            return p.astype(jnp.bfloat16).astype(jnp.float32)

        def body(step, carry):
            for sub in range(group):
                c = step * group + sub
                total = product(sides[0], c)
                for side in sides[1:]:
                    total = total + product(side, c)
                acc[c] = total if first else acc[c] + total
            return carry

        with jax.named_scope(f'stage{d}_{len(sides)}{sides[0]}_{lo}'):
            lax.fori_loop(lo // group, hi // group, body, 0)

    def ready(d):
        take_twin = twin[d].at[pl.ds(0, nb + na)]
        with jax.named_scope(f'ready{d}'):
            pltpu.make_async_copy(take_twin, take_twin, drecv.at[d]).wait()

    def y_taken(cols, k):
        u, v, size = lay(k, theirs)
        arrive(("y", cols, k), 2 * size * len(cols))
        for d in cols:
            share(d, u, size)
            share(d, v, size)

    near = (LEFT, RIGHT)
    third = nc // 3

    for n, pair in enumerate(w_pieces):
        arrive(("xw", n), sum(size for _, size, _ in pair))
        for link, d, (off, size, goes_on) in zip(("x+", "x-"), (LEFT, RIGHT), pair):
            send("y+", ("yw", near), d, d, q0 + off, size)
            send("y-", ("yw", near), d, d, q0 + off, size)
            if goes_on:
                send(link, ("f", "w"), d, FAR, q0 + off, size)
            share(d, q0 + off, size)
    share(0, 0, nb + na)

    def spread(k):
        (up, up_size), (down, down_size) = parts if k == 0 else parts[::-1]
        for d in (near if k == 0 else (FAR,)):
            send("y+", ("g", k), d, d, qm + up, up_size)
            send("y-", ("g", k), d, d, qp + down, down_size)
            share(d, qm, quad)
            share(d, qp, quad)

    for k in range(nk):
        u, v, size = lay(k, own)
        if k == nk - 1:
            for part in range(2):
                send("x+", ("a", part), 0, LEFT, nb + part * ah, ah)
                send("x-", ("a", part), 0, RIGHT, nb + (1 - part) * ah, ah)
        arrive(("x", k, 0), 2 * size)
        send("y+", ("y", near, k), LEFT, LEFT, u, size)
        send("x+", ("f", k), LEFT, FAR, u, size)
        send("y-", ("y", near, k), RIGHT, RIGHT, v, size)
        send("x-", ("f", k), RIGHT, FAR, v, size)
        share(LEFT, u, size)
        share(RIGHT, v, size)
        if k == 0:
            lists_taken(RING - 1, 1)
            for d in range(1, RING):
                list_to(2 * d + 1, 2 * d, sib, 2)
        elif k == 1:
            arrive(("yw", near), 4 * quad)
            spread(0)
        elif k == 2:
            stage(0, lo=third, hi=2 * third, first=True)
            y_taken(near, 0)
        elif k == 3:
            y_taken(near, 1)
        arrive(("x", k, 1), 2 * size)
        send("y-", ("y", near, k), LEFT, LEFT, v, size)
        send("y+", ("y", near, k), RIGHT, RIGHT, u, size)
        share(LEFT, v, size)
        share(RIGHT, u, size)
        if k == 0:
            build_table()
        elif k == 1:
            pltpu.make_async_copy(tab_v, tab_s, loc_sem.at[3]).wait()
            ready(0)
            stage(0, hi=third, first=True)
        elif k == 2:
            stage(0, lo=2 * third, first=True)
    arrive(("g", 0), 2 * quad)
    for d in near:
        share(d, qf, quad)

    def far_block(k):
        u, v, size = lay(k, own)
        arrive(("f", k), 2 * size)
        send("y+", ("y", (FAR,), k), FAR, FAR, u, size)
        send("y-", ("y", (FAR,), k), FAR, FAR, v, size)
        share(FAR, u, size)
        share(FAR, v, size)

    arrive(("f", "w"), quad)
    send("y+", ("yw", FAR), FAR, FAR, q0, quad)
    send("y-", ("yw", FAR), FAR, FAR, q0, quad)
    share(FAR, q0, quad)
    y_taken(near, 2)
    far_block(0)
    far_block(1)
    y_taken(near, 3)
    far_block(2)
    y_taken(near, 4)
    far_block(3)
    arrive(("yw", FAR), 2 * quad)
    spread(1)
    y_taken((FAR,), 0)

    arrive(("a", 0), 2 * ah)
    send("x+", ("f", "a"), LEFT, FAR, nb, ah)
    send("x-", ("f", "a"), RIGHT, FAR, nb + ah, ah)
    share(LEFT, nb, ah)
    share(RIGHT, nb + ah, ah)
    arrive(("a", 1), 2 * ah)
    share(LEFT, nb + ah, ah)
    share(RIGHT, nb, ah)
    stage(LEFT, (0,))
    far_block(4)
    y_taken((FAR,), 1)
    ready(LEFT)
    stage(LEFT, (1,))
    y_taken((FAR,), 2)
    ready(RIGHT)
    stage(RIGHT)
    arrive(("g", 1), quad)
    share(FAR, qf, quad)
    y_taken((FAR,), 3)
    arrive(("f", "a"), 2 * ah)
    share(FAR, nb, na)
    y_taken((FAR,), 4)
    stage(FAR, (0,), group=nc // 2)
    ready(FAR)
    stage(FAR, (1,), hi=head)

    assert load_of == waited and len(sems) == recv_sem.shape[0], len(sems)
    with jax.named_scope('sendwaits'):
        for slot, size in enumerate(link_of):
            take(size, link_sem.at[slot])
        own_meta = meta.at[pl.ds(0, 2 * RING - 1)]
        pltpu.make_async_copy(own_meta, own_meta, msem.at[0]).wait()
        for d in range(RING):
            take(nb + na, dsend.at[d])


def finish(head, cuts, acc, far, tab, out_hbm, buf, tab_s, tab_sem, out_sem):
    table = pltpu.make_async_copy(tab, tab_s, tab_sem)
    table.start()
    first = pl.ds(0, head)
    outs, lo = [pltpu.make_async_copy(acc.at[first], out_hbm.at[first], out_sem.at[len(cuts)])], head
    outs[0].start()
    table.wait()
    for n, hi in enumerate(cuts):
        for c in range(lo, hi):
            p = jnp.dot(far[tab_s[0, c]], far[tab_s[1, c]], preferred_element_type=jnp.float32)
            buf[c] = acc[c] + p.astype(jnp.bfloat16).astype(jnp.float32)
        view = pl.ds(lo, hi - lo)
        outs.append(pltpu.make_async_copy(buf.at[view], out_hbm.at[view], out_sem.at[n]))
        outs[-1].start()
        lo = hi
    for copy in outs:
        copy.wait()


def solution(mesh):
    row_spec = P(('batch', 'rows'), 'ksplit')
    col_spec = P(('batch', 'ksplit'))
    assert mesh.shape['rows'] == RING and mesh.shape['ksplit'] == 2 * RING

    def device_step(a_loc, b_loc, pair_loc, plist_loc, cidx_loc):
        a, b = a_loc[0, 0], b_loc[0]
        pairs = pair_loc[0, 0, :, 0, :].T
        plist = plist_loc[0, 0].T
        cidx = cidx_loc[0, 0].T
        na, nb, nc, size = a.shape[0], b.shape[0], cidx.shape[1], a.shape[-1]
        npart = plist.shape[1]
        nsem = 11 + 5 * len(HALF_CHUNKS)
        block = (size, size)
        args = [pltpu.with_memory_space_constraint(t, pltpu.HBM) for t in (a, b, pairs, plist, cidx)]
        head = nc // 3
        acc, far, tab = pl.pallas_call(
            functools.partial(kernel, na, nb, nc, head),
            out_shape=(
                jax.ShapeDtypeStruct((nc, *block), jnp.float32),
                jax.ShapeDtypeStruct((nb + na + 1, *block), b.dtype),
                jax.ShapeDtypeStruct((2, 128), jnp.int32),
            ),
            in_specs=[pl.BlockSpec(memory_space=pltpu.HBM)] * 5,
            out_specs=(pl.BlockSpec(memory_space=pltpu.VMEM),) * 3,
            scratch_shapes=[
                *[pltpu.VMEM((nb + na + 1, *block), b.dtype) for _ in range(2 * RING - 1)],
                pltpu.VMEM((2 * RING, 2, 2, npart), jnp.int32),
                pltpu.VMEM((2, nc), jnp.int32),
                pltpu.VMEM((nc, 128), jnp.int32),
                pltpu.SMEM((nc, 128), jnp.int32),
                pltpu.SemaphoreType.DMA((4,)),
                pltpu.SemaphoreType.DMA((4,)),
                pltpu.SemaphoreType.DMA((nsem,)),
                pltpu.SemaphoreType.DMA((RING,)),
                pltpu.SemaphoreType.DMA((RING,)),
                pltpu.SemaphoreType.DMA((3,)),
            ],
            compiler_params=pltpu.CompilerParams(
                collective_id=0, has_side_effects=True, vmem_limit_bytes=30 * 2**20),
        )(*args)
        cuts = tuple(head + (nc - head) * n // 6 for n in (2, 4, 5, 6))
        vmem = pl.BlockSpec(memory_space=pltpu.VMEM)
        out = pl.pallas_call(
            functools.partial(finish, head, cuts),
            out_shape=jax.ShapeDtypeStruct((nc, *block), jnp.float32),
            in_specs=[vmem] * 3,
            out_specs=pl.BlockSpec(memory_space=pltpu.HBM),
            scratch_shapes=[
                pltpu.VMEM((nc, *block), jnp.float32),
                pltpu.SMEM((2, 128), jnp.int32),
                pltpu.SemaphoreType.DMA,
                pltpu.SemaphoreType.DMA((len(cuts) + 1,)),
            ],
            compiler_params=pltpu.CompilerParams(vmem_limit_bytes=8 * 2**20),
        )(acc, far, tab)
        return out[None, None]

    return jax.shard_map(device_step, mesh=mesh, in_specs=(row_spec, col_spec, row_spec, row_spec, row_spec), out_specs=row_spec, check_vma=False)
```

profile of v0, /device:TPU:97, one launch (start us, length us, event | category | flops | bytes accessed | tf_op | source)
XLA Modules:
  0.0 60.4 jit_solution(7467532160320051334)
XLA Ops:
  0.0 57.8 %shard_map.55 = (f32[72,128,128]{2,1,0:T(8,128)S(1)}, bf16[85,128,128]{2,1,0:T(8,128)(2,1)S(1)}, s32[2,128]{1,0:T(2,128)S(1)}) custom-call(bf16[12,128,128]{2,1,0:T(8,128)(2,1)} %bitcast.13, bf16[72,128,128]{2,1,0:T(8,128)(2,1)} %bitcast.12, s32[2,432]{1,0:T(2,128)} %bitcast.14, s32[2,432]{1,0:T(2,128)} %bitcast.15, s32[2,72]{1,0:T(2,128)} %bitcast.16), custom_call_target="tpu_custom_call" | custom-call | tf_op jit(solution)/shard_map/pallas_call | solution.py:355
  57.8 2.6 %shard_map.56 = f32[72,128,128]{2,1,0:T(8,128)} custom-call(f32[72,128,128]{2,1,0:T(8,128)S(1)} %get-tuple-element.8.acc, bf16[85,128,128]{2,1,0:T(8,128)(2,1)S(1)} %get-tuple-element.9.far, s32[2,128]{1,0:T(2,128)S(1)} %get-tuple-element.10.tab), custom_call_target="tpu_custom_call" | custom-call | tf_op jit(solution)/shard_map/pallas_call | solution.py:382
where the time goes:
time: 60.5 us; the launch traced here: 60.4 us
  Pallas kernels  60.4 us (100%)
    pallas_call x1, Pallas kernels, device_step(): pl.pallas_call(functools.partial(kernel, na, nb, nc, head), out_shape=(ja...  57.8 us
    pallas_call x1, Pallas kernels, device_step(): pl.pallas_call(functools.partial(finish, head, cuts), out_shape=jax.Shape...  2.58 us

commit v1 on v0

--- a/solution.py
+++ b/solution.py
@@ -320,17 +320,23 @@
 def finish(head, cuts, acc, far, tab, out_hbm, buf, tab_s, tab_sem, out_sem):
     table = pltpu.make_async_copy(tab, tab_s, tab_sem)
     table.start()
-    first = pl.ds(0, head)
-    outs, lo = [pltpu.make_async_copy(acc.at[first], out_hbm.at[first], out_sem.at[len(cuts)])], head
-    outs[0].start()
+    outs = []
+
+    def write(src, lo, hi):
+        view, n = pl.ds(lo, hi - lo), len(outs)
+        outs.append(pltpu.make_async_copy(src.at[view], out_hbm.at[view], out_sem.at[n]))
+        outs[-1].start(priority=n % 2)
+
+    step = cuts[0] - head
+    for lo in range(0, head, step):
+        write(acc, lo, lo + step)
     table.wait()
-    for n, hi in enumerate(cuts):
+    lo = head
+    for hi in cuts:
         for c in range(lo, hi):
             p = jnp.dot(far[tab_s[0, c]], far[tab_s[1, c]], preferred_element_type=jnp.float32)
             buf[c] = acc[c] + p.astype(jnp.bfloat16).astype(jnp.float32)
-        view = pl.ds(lo, hi - lo)
-        outs.append(pltpu.make_async_copy(buf.at[view], out_hbm.at[view], out_sem.at[n]))
-        outs[-1].start()
+        write(buf, lo, hi)
         lo = hi
     for copy in outs:
         copy.wait()
@@ -377,7 +383,7 @@
             compiler_params=pltpu.CompilerParams(
                 collective_id=0, has_side_effects=True, vmem_limit_bytes=30 * 2**20),
         )(*args)
-        cuts = tuple(head + (nc - head) * n // 6 for n in (2, 4, 5, 6))
+        cuts = tuple(head + (nc - head) * n // 6 for n in range(1, 7))
         vmem = pl.BlockSpec(memory_space=pltpu.VMEM)
         out = pl.pallas_call(
             functools.partial(finish, head, cuts),
@@ -388,7 +394,7 @@
                 pltpu.VMEM((nc, *block), jnp.float32),
                 pltpu.SMEM((2, 128), jnp.int32),
                 pltpu.SemaphoreType.DMA,
-                pltpu.SemaphoreType.DMA((len(cuts) + 1,)),
+                pltpu.SemaphoreType.DMA((len(cuts) + 3,)),
             ],
             compiler_params=pltpu.CompilerParams(vmem_limit_bytes=8 * 2**20),
         )(acc, far, tab)

time: 60.5 us -> 60.4 us (level)
  no operation moved by 1% of the time
where the time goes in v1:
time: 60.4 us; the launch traced here: 60.3 us
  Pallas kernels  60.3 us (100%)
    pallas_call x1, Pallas kernels, device_step(): pl.pallas_call(functools.partial(kernel, na, nb, nc, head), out_shape=(ja...  57.8 us
    pallas_call x1, Pallas kernels, device_step(): pl.pallas_call(functools.partial(finish, head, cuts), out_shape=jax.Shape...  2.52 us

profile of v1, /device:TPU:97, one launch (start us, length us, event | category | flops | bytes accessed | tf_op | source)
XLA Modules:
  0.0 60.3 jit_solution(14653163911987242340)
XLA Ops:
  0.0 57.8 %shard_map.55 = (f32[72,128,128]{2,1,0:T(8,128)S(1)}, bf16[85,128,128]{2,1,0:T(8,128)(2,1)S(1)}, s32[2,128]{1,0:T(2,128)S(1)}) custom-call(bf16[12,128,128]{2,1,0:T(8,128)(2,1)} %bitcast.13, bf16[72,128,128]{2,1,0:T(8,128)(2,1)} %bitcast.12, s32[2,432]{1,0:T(2,128)} %bitcast.14, s32[2,432]{1,0:T(2,128)} %bitcast.15, s32[2,72]{1,0:T(2,128)} %bitcast.16), custom_call_target="tpu_custom_call" | custom-call | tf_op jit(solution)/shard_map/pallas_call | solution.py:361
  57.8 2.5 %shard_map.56 = f32[72,128,128]{2,1,0:T(8,128)} custom-call(f32[72,128,128]{2,1,0:T(8,128)S(1)} %get-tuple-element.8.acc, bf16[85,128,128]{2,1,0:T(8,128)(2,1)S(1)} %get-tuple-element.9.far, s32[2,128]{1,0:T(2,128)S(1)} %get-tuple-element.10.tab), custom_call_target="tpu_custom_call" | custom-call | tf_op jit(solution)/shard_map/pallas_call | solution.py:388
